TPU v7x, 256 devices: a whole 4x4x8 slice. The times are simulated.
256 devices in a mesh: ep: 32 (over z_lo, y, x), dp: 8 (over z_hi, core).
Axes of the slice: x: 4, y: 4, z: 8 (z_hi: 4, z_lo: 2; z = z_hi * 2 + z_lo), core: 2. Of those that a mesh axis runs over, the one named last changes fastest.
Arguments:
- tokens: bfloat16 [16384, 2048], P(('dp', 'ep')), parts along dimension 0, may hold values from -6 to 6
- expert_ids: int32 [16384, 8], P(('dp', 'ep')), parts along dimension 0, may hold values from 0 to 31, all different within a row; in each aligned block of 64 rows (0 to 63, 64 to 127, ...) at most 32 rows name the same one
- gate_probs: float32 [16384, 8], P(('dp', 'ep')), parts along dimension 0, may hold values from 0.05 to 1
- w_gate: bfloat16 [32, 2048, 768], P('ep'), may hold values from -0.125 to 0.125
- w_up: bfloat16 [32, 2048, 768], P('ep'), may hold values from -0.125 to 0.125
- w_down: bfloat16 [32, 768, 2048], P('ep'), may hold values from -0.21875 to 0.21875
Outputs:
- combined: bfloat16 [16384, 2048], P(('dp', 'ep')), parts along dimension 0
There are 8 independent parts, one for each index of `dp`. A program takes and returns all parts, laid end to end along the dimension named above; an argument that names none is the same for every part. Nothing has to cross between parts.
Inputs may be any that keep to these rules, and one draw needn't show every extreme that they name: `expert_ids`: each row names 8 different experts. Among the rows of one index of ep (aligned blocks of 64 rows) no expert is named by more than 32 rows, and in every draw some expert is named by exactly 32 rows of some block. Expert popularity is skewed.
All inputs are finite; a program needn't handle non-finite values.
Results may differ from a plain program's by a relative error of at most 0.0085.
Values may be sent and summed in bfloat16 or wider, within the bound.
No kernel may reach another device: no remote copies, remote signals or barrier semaphores. Data moves between devices by JAX's collectives and lax.ppermute only.
A program may use at most 64 MiB of HBM per device.

v0:
```python
import jax
import jax.numpy as jnp
from jax import lax
from jax.experimental import pallas as pl
from jax.experimental.pallas import tpu as pltpu
from jax.sharding import Mesh, PartitionSpec as P


F32 = jnp.float32
BF16 = jnp.bfloat16
CAP = 32
SIDE = 4
EXPERTS = 32
META = 128
SLOTS = SIDE * CAP
NONE = 255.0
VMEM = pl.BlockSpec(memory_space=pltpu.VMEM)
PARAMS = pltpu.CompilerParams(vmem_limit_bytes=48 * 1024 * 1024)


def prep_kernel(tok_hbm, ids_hbm, prob_hbm, out_ref, ids_ref, prob_ref, sems):
    rows, features = tok_hbm.shape
    top = ids_hbm.shape[0]
    pairs = ((ids_hbm, ids_ref), (prob_hbm, prob_ref), (tok_hbm, out_ref.at[:, :features]))
    copies = [pltpu.make_async_copy(a, b, sems.at[i]) for i, (a, b) in enumerate(pairs)]
    for copy in copies:
        copy.start()
    copies[0].wait()
    copies[1].wait()
    prob = prob_ref[...]
    weight = (prob / jnp.sum(prob, axis=0, keepdims=True)).T
    ids = ids_ref[...].astype(F32).T
    lane = lax.broadcasted_iota(jnp.int32, (rows, META), 1)
    expert = (lane % EXPERTS).astype(F32)
    named = jnp.zeros((rows, META), F32)
    value = jnp.zeros((rows, META), F32)
    for k in range(top):
        hit = ids[:, k : k + 1] == expert
        named = jnp.where(hit, 1.0, named)
        value = jnp.where(hit, weight[:, k : k + 1], value)
    before = (
        lax.broadcasted_iota(jnp.int32, (rows, rows), 0) > lax.broadcasted_iota(jnp.int32, (rows, rows), 1)
    ).astype(F32).astype(BF16)
    rank = jnp.dot(before, named.astype(BF16), preferred_element_type=F32)
    slot = jnp.where(named > 0.0, rank, NONE)
    high = value.astype(BF16).astype(F32)
    part = lane // EXPERTS
    meta = jnp.where(part == 0, slot, jnp.where(part == 1, high, value - high))
    out_ref[:, features:] = meta.astype(BF16)
    copies[2].wait()


def pack_kernel(owner_ref, *refs):
    blocks, outs, weights_ref = refs[:SIDE], refs[SIDE : 2 * SIDE], refs[2 * SIDE]
    rows, width = blocks[0].shape
    features = width - META
    owner = owner_ref[...]
    source = lax.broadcasted_iota(jnp.int32, (META, SLOTS), 0)
    pick = [(source == owner + part * EXPERTS).astype(F32).astype(BF16) for part in range(3)]
    place = (lax.broadcasted_iota(jnp.int32, (rows, SLOTS), 1) % CAP).astype(F32)
    for b in range(SIDE):
        meta = blocks[b][:, features:]
        slot, high, low = (jnp.dot(meta, p, preferred_element_type=F32) for p in pick)
        chosen = slot == place
        weights_ref[b, :, :SLOTS] = jnp.where(chosen, high, 0.0).astype(BF16)
        weights_ref[b, :, SLOTS:] = jnp.where(chosen, low, 0.0).astype(BF16)
        table = jnp.where(chosen, 1.0, 0.0).T.astype(BF16)
        picked = jnp.dot(table, blocks[b][:, :features], preferred_element_type=F32).astype(BF16)
        for d in range(SIDE):
            outs[d][b * CAP : (b + 1) * CAP, :] = picked[d * CAP : (d + 1) * CAP, :]


def unpack_kernel(weights_ref, *refs):
    rows_in, outs = refs[:SIDE], refs[SIDE : 2 * SIDE]
    for b in range(SIDE):
        stacked = jnp.concatenate([r[b * CAP : (b + 1) * CAP, :] for r in rows_in], axis=0)
        total = jnp.dot(weights_ref[b, :, :SLOTS], stacked, preferred_element_type=F32)
        total = total + jnp.dot(weights_ref[b, :, SLOTS:], stacked, preferred_element_type=F32)
        outs[b][...] = total.astype(BF16)


def ffn_kernel(gate_ref, up_ref, down_ref, *refs):
    rows_in, outs, held, hidden = refs[:SIDE], refs[SIDE : 2 * SIDE], refs[2 * SIDE], refs[2 * SIDE + 1]
    height = rows_in[0].shape[0]
    inner = gate_ref.shape[2]
    features = down_ref.shape[2]
    for d in range(SIDE):
        held[d * height : (d + 1) * height, :] = rows_in[d][...]
    tile = 256
    for t in range(inner // tile):
        cols = slice(t * tile, (t + 1) * tile)
        gate = jnp.dot(held[...], gate_ref[0, :, cols], preferred_element_type=F32)
        up = jnp.dot(held[...], up_ref[0, :, cols], preferred_element_type=F32)
        hidden[:, cols] = (gate / (1.0 + jnp.exp(-gate)) * up).astype(BF16)
    for t in range(features // tile):
        cols = slice(t * tile, (t + 1) * tile)
        out = jnp.dot(hidden[...], down_ref[0, :, cols], preferred_element_type=F32).astype(BF16)
        for d in range(SIDE):
            outs[d][:, cols] = out[d * height : (d + 1) * height, :]


def call(kernel, shapes, *args, scratch=(), space=pltpu.VMEM):
    return pl.pallas_call(
        kernel,
        out_shape=shapes,
        in_specs=[pl.BlockSpec(memory_space=space)] * len(args),
        out_specs=jax.tree.map(lambda _: VMEM, shapes),
        scratch_shapes=scratch,
        compiler_params=PARAMS,
    )(*args)


STEPS = (1, 3, 2)


def shift(value, axis, by):
    count = lax.axis_size(axis)
    return lax.ppermute(value, axis, [(i, (i + by) % count) for i in range(count)])


def shift_all(values, axis, sign):
    out = [values[0]] + [None] * (SIDE - 1)
    for d in STEPS:
        out[d] = shift(values[d], axis, sign * d)
    return out


def shards(tokens, expert_ids, gate_probs, w_gate, w_up, w_down):
    count, features = tokens.shape
    top = expert_ids.shape[1]
    inner = w_gate.shape[2]
    z, y, x = (lax.axis_index(n) for n in "zyx")
    step = (jnp.arange(SLOTS, dtype=jnp.int32) // CAP)[None, :]
    base = z * SIDE * SIDE
    owners = (base + y * SIDE + (x + step) % SIDE, base + (y + step) % SIDE * SIDE + x)
    shape = jax.ShapeDtypeStruct

    mine = call(
        prep_kernel, shape((count, features + META), BF16), tokens, expert_ids.T, gate_probs.T,
        space=pltpu.HBM,
        scratch=[pltpu.VMEM((top, count), jnp.int32), pltpu.VMEM((top, count), F32), pltpu.SemaphoreType.DMA((3,))],
    )
    theirs = shift(mine, "z", 1)
    pack_shapes = [shape((SLOTS, features), BF16)] * SIDE + [shape((SIDE, count, 2 * SLOTS), BF16)]
    unpack_shapes = [shape((count, features), BF16)] * SIDE
    ffn_shapes = [shape((SLOTS, features), BF16)] * SIDE
    height = SIDE * SLOTS
    scratch = [pltpu.VMEM((height, features), BF16), pltpu.VMEM((height, inner), BF16)]

    partial = []
    for block, owner, first, last in ((mine, owners[0], "y", "x"), (theirs, owners[1], "x", "y")):
        gathered = shift_all([block] * SIDE, first, 1)
        *packed, weights = call(pack_kernel, pack_shapes, owner, *gathered)
        arrived = shift_all(packed, last, 1)
        served = call(ffn_kernel, ffn_shapes, w_gate, w_up, w_down, *arrived, scratch=scratch)
        back = shift_all(served, last, -1)
        summed = call(unpack_kernel, unpack_shapes, weights, *back)
        partial.append(sum(p.astype(F32) for p in shift_all(summed, first, -1)))
    own, other = partial
    return (own + shift(other.astype(BF16), "z", 1).astype(F32)).astype(BF16)


def solution(mesh):
    grid = Mesh(mesh.devices.reshape(2, SIDE, SIDE, 4, 2), ("z", "y", "x", "h", "c"))
    rows = P(("h", "c", "z", "y", "x"), None)
    owner = P(("z", "y", "x"), None, None)

    return jax.shard_map(
        shards, mesh=grid, in_specs=(rows, rows, rows, owner, owner, owner), out_specs=rows, check_vma=False
    )
```

profile of v0, /device:TPU:64, one launch (start us, length us, event | category | flops | bytes accessed | tf_op | source)
XLA Modules:
  0.0 138.8 jit_solution(10907765721108494742)
XLA Ops:
  0.0 0.9 copy-done
  1.0 0.7 copy-done.1
  1.6 0.7 copy-done.2
  2.3 0.5 shard_map.64.refs_0_
  2.8 2.0 %collective-permute-start.12 = (bf16[64,2176]{1,0:T(8,128)(2,1)S(1)}, bf16[64,2176]{1,0:T(8,128)(2,1)S(1)}, u32[]{:S(2)}, u32[]{:S(2)}) collective-permute-start(bf16[64,2176]{1,0:T(8,128)(2,1)S(1)} %shard_map.64.refs_0_), channel_id=1, source_target_pairs={{0,128},{128,0},{1,129},{129,1},{2,130},{130,2},{3,131},{131,3},{4... | collective-permute-start | bytes 835592 | tf_op jit(solution)/shard_map/ppermute | solution.py:118
  4.8 6.7 %collective-permute-done.12.refs_0_ = bf16[64,2176]{1,0:T(8,128)(2,1)S(1)} collective-permute-done((bf16[64,2176]{1,0:T(8,128)(2,1)S(1)}, bf16[64,2176]{1,0:T(8,128)(2,1)S(1)}, u32[]{:S(2)}, u32[]{:S(2)}) %collective-permute-start.12) | collective-permute-done | bytes 278560 | tf_op jit(solution)/shard_map/ppermute | solution.py:118
  11.5 1.5 %collective-permute-start.13 = (bf16[64,2176]{1,0:T(8,128)(2,1)S(1)}, bf16[64,2176]{1,0:T(8,128)(2,1)S(1)}, u32[]{:S(2)}, u32[]{:S(2)}) collective-permute-start(bf16[64,2176]{1,0:T(8,128)(2,1)S(1)} %collective-permute-done.12.refs_0_), channel_id=1, source_target_pairs={{0,8},{8,16},{16,24},{24,0},{1,9},{9,17},{17,25},{25,1},{2,10},{10... | collective-permute-start | bytes 835592 | tf_op jit(solution)/shard_map/ppermute | solution.py:118
  13.0 2.7 %collective-permute-start.14 = (bf16[64,2176]{1,0:T(8,128)(2,1)S(1)}, bf16[64,2176]{1,0:T(8,128)(2,1)S(1)}, u32[]{:S(2)}, u32[]{:S(2)}) collective-permute-start(bf16[64,2176]{1,0:T(8,128)(2,1)S(1)} %collective-permute-done.12.refs_0_), channel_id=1, source_target_pairs={{0,16},{8,24},{16,0},{24,8},{1,17},{9,25},{17,1},{25,9},{2,18},{10... | collective-permute-start | bytes 835592 | tf_op jit(solution)/shard_map/ppermute | solution.py:118
  15.7 1.4 %collective-permute-start.15 = (bf16[64,2176]{1,0:T(8,128)(2,1)S(1)}, bf16[64,2176]{1,0:T(8,128)(2,1)S(1)}, u32[]{:S(2)}, u32[]{:S(2)}) collective-permute-start(bf16[64,2176]{1,0:T(8,128)(2,1)S(1)} %collective-permute-done.12.refs_0_), channel_id=1, source_target_pairs={{0,24},{8,0},{16,8},{24,16},{1,25},{9,1},{17,9},{25,17},{2,26},{10... | collective-permute-start | bytes 835592 | tf_op jit(solution)/shard_map/ppermute | solution.py:118
  17.1 1.6 %collective-permute-start = (bf16[64,2176]{1,0:T(8,128)(2,1)S(1)}, bf16[64,2176]{1,0:T(8,128)(2,1)S(1)}, u32[]{:S(2)}, u32[]{:S(2)}) collective-permute-start(bf16[64,2176]{1,0:T(8,128)(2,1)S(1)} %shard_map.64.refs_0_), channel_id=1, source_target_pairs={{0,32},{32,64},{64,96},{96,0},{1,33},{33,65},{65,97},{97,1},{2,34}... | collective-permute-start | bytes 835592 | tf_op jit(solution)/shard_map/ppermute | solution.py:118
  18.7 2.5 %collective-permute-done.13.refs_1_ = bf16[64,2176]{1,0:T(8,128)(2,1)S(1)} collective-permute-done((bf16[64,2176]{1,0:T(8,128)(2,1)S(1)}, bf16[64,2176]{1,0:T(8,128)(2,1)S(1)}, u32[]{:S(2)}, u32[]{:S(2)}) %collective-permute-start.13) | collective-permute-done | bytes 278560 | tf_op jit(solution)/shard_map/ppermute | solution.py:118
  21.2 6.1 %collective-permute-done.14.refs_2_ = bf16[64,2176]{1,0:T(8,128)(2,1)S(1)} collective-permute-done((bf16[64,2176]{1,0:T(8,128)(2,1)S(1)}, bf16[64,2176]{1,0:T(8,128)(2,1)S(1)}, u32[]{:S(2)}, u32[]{:S(2)}) %collective-permute-start.14) | collective-permute-done | bytes 278560 | tf_op jit(solution)/shard_map/ppermute | solution.py:118
  27.3 0.0 collective-permute-done.15.refs_3_
  27.3 2.7 %shard_map.68 = (bf16[128,2048]{1,0:T(8,128)(2,1)S(1)}, bf16[128,2048]{1,0:T(8,128)(2,1)}, bf16[128,2048]{1,0:T(8,128)(2,1)}, bf16[128,2048]{1,0:T(8,128)(2,1)}, bf16[4,64,256]{2,1,0:T(8,128)(2,1)S(1)}) custom-call(s32[1,128]{1,0:T(1,128)S(1)} %fusion.3.owner_ref, bf16[64,2176]{1,0:T(8,128)(2,1)S(1)} %collective-permute-done.12.refs_0_, ...), custom_call_target="tpu_custom_call" | custom-call | tf_op jit(solution)/shard_map/pallas_call | solution.py:103
  30.0 1.6 %collective-permute-start.16 = (bf16[128,2048]{1,0:T(8,128)(2,1)}, bf16[128,2048]{1,0:T(8,128)(2,1)S(1)}, u32[]{:S(2)}, u32[]{:S(2)}) collective-permute-start(bf16[128,2048]{1,0:T(8,128)(2,1)} %get-tuple-element.46), channel_id=1, source_target_pairs={{0,32},{32,64},{64,96},{96,0},{1,33},{33,65},{65,97},{97,1},{2,34}... | collective-permute-start | bytes 1572872 | tf_op jit(solution)/shard_map/ppermute | solution.py:118
  31.6 2.9 %collective-permute-start.1 = (bf16[64,2176]{1,0:T(8,128)(2,1)S(1)}, bf16[64,2176]{1,0:T(8,128)(2,1)S(1)}, u32[]{:S(2)}, u32[]{:S(2)}) collective-permute-start(bf16[64,2176]{1,0:T(8,128)(2,1)S(1)} %shard_map.64.refs_0_), channel_id=1, source_target_pairs={{0,64},{32,96},{64,0},{96,32},{1,65},{33,97},{65,1},{97,33},{2,66}... | collective-permute-start | bytes 835592 | tf_op jit(solution)/shard_map/ppermute | solution.py:118
  34.5 1.3 collective-permute-start.2
  35.8 0.3 collective-permute-start.17
  36.2 0.0 collective-permute-done.refs_1_
  36.2 3.0 %collective-permute-start.18 = (bf16[128,2048]{1,0:T(8,128)(2,1)}, bf16[128,2048]{1,0:T(8,128)(2,1)S(1)}, u32[]{:S(2)}, u32[]{:S(2)}) collective-permute-start(bf16[128,2048]{1,0:T(8,128)(2,1)} %get-tuple-element.48), channel_id=1, source_target_pairs={{0,96},{32,0},{64,32},{96,64},{1,97},{33,1},{65,33},{97,65},{2,98}... | collective-permute-start | bytes 1572872 | tf_op jit(solution)/shard_map/ppermute | solution.py:118
  39.2 14.2 %collective-permute-done.1.refs_2_ = bf16[64,2176]{1,0:T(8,128)(2,1)S(1)} collective-permute-done((bf16[64,2176]{1,0:T(8,128)(2,1)S(1)}, bf16[64,2176]{1,0:T(8,128)(2,1)S(1)}, u32[]{:S(2)}, u32[]{:S(2)}) %collective-permute-start.1) | collective-permute-done | bytes 278560 | tf_op jit(solution)/shard_map/ppermute | solution.py:118
  53.4 0.2 collective-permute-done.2.refs_3_
  53.6 1.5 %shard_map.65 = (bf16[128,2048]{1,0:T(8,128)(2,1)S(1)}, bf16[128,2048]{1,0:T(8,128)(2,1)S(1)}, bf16[128,2048]{1,0:T(8,128)(2,1)S(1)}, bf16[128,2048]{1,0:T(8,128)(2,1)S(1)}, bf16[4,64,256]{2,1,0:T(8,128)(2,1)S(1)}) custom-call(s32[1,128]{1,0:T(1,128)S(1)} %fusion.owner_ref, bf16[64,2176]{1,0:T(8,128)(2,1)S(1)} %shard_map.64.refs_0_, ...), custom_call_target="tpu_custom_call" | custom-call | tf_op jit(solution)/shard_map/pallas_call | solution.py:103
  55.1 1.3 collective-permute-start.3
  56.4 2.4 %collective-permute-start.4 = (bf16[128,2048]{1,0:T(8,128)(2,1)S(1)}, bf16[128,2048]{1,0:T(8,128)(2,1)S(1)}, u32[]{:S(2)}, u32[]{:S(2)}) collective-permute-start(bf16[128,2048]{1,0:T(8,128)(2,1)S(1)} %get-tuple-element.34), channel_id=1, source_target_pairs={{0,16},{8,24},{16,0},{24,8},{1,17},{9,25},{17,1},{25,9},{2,18},{10... | collective-permute-start | bytes 1572872 | tf_op jit(solution)/shard_map/ppermute | solution.py:118
  58.8 0.0 collective-permute-done.16.refs_1_
  58.8 1.8 %collective-permute-start.5 = (bf16[128,2048]{1,0:T(8,128)(2,1)S(1)}, bf16[128,2048]{1,0:T(8,128)(2,1)S(1)}, u32[]{:S(2)}, u32[]{:S(2)}) collective-permute-start(bf16[128,2048]{1,0:T(8,128)(2,1)S(1)} %get-tuple-element.35), channel_id=1, source_target_pairs={{0,24},{8,0},{16,8},{24,16},{1,25},{9,1},{17,9},{25,17},{2,26},{10... | collective-permute-start | bytes 1572872 | tf_op jit(solution)/shard_map/ppermute | solution.py:118
  60.5 1.7 %collective-permute-done.17.refs_2_ = bf16[128,2048]{1,0:T(8,128)(2,1)S(1)} collective-permute-done((bf16[128,2048]{1,0:T(8,128)(2,1)}, bf16[128,2048]{1,0:T(8,128)(2,1)S(1)}, u32[]{:S(2)}, u32[]{:S(2)}) %collective-permute-start.17) | collective-permute-done | bytes 524320 | tf_op jit(solution)/shard_map/ppermute | solution.py:118
  62.2 5.2 %collective-permute-done.18.refs_3_ = bf16[128,2048]{1,0:T(8,128)(2,1)S(1)} collective-permute-done((bf16[128,2048]{1,0:T(8,128)(2,1)}, bf16[128,2048]{1,0:T(8,128)(2,1)S(1)}, u32[]{:S(2)}, u32[]{:S(2)}) %collective-permute-start.18) | collective-permute-done | bytes 524320 | tf_op jit(solution)/shard_map/ppermute | solution.py:118
  67.4 8.8 %shard_map.69 = (bf16[128,2048]{1,0:T(8,128)(2,1)S(1)}, bf16[128,2048]{1,0:T(8,128)(2,1)S(1)}, bf16[128,2048]{1,0:T(8,128)(2,1)S(1)}, bf16[128,2048]{1,0:T(8,128)(2,1)S(1)}) custom-call(bf16[1,2048,768]{2,1,0:T(8,128)(2,1)} %gate_ref.3, bf16[1,2048,768]{2,1,0:T(8,128)(2,1)} %up_ref.3, bf16[1,768,2048]{2,1,0:T(8,128)(2,1)} %down_ref.3, ...), custom_call_target="tpu_custom_call" | custom-call | tf_op jit(solution)/shard_map/pallas_call | solution.py:103
  76.2 2.7 %collective-permute-start.19 = (bf16[128,2048]{1,0:T(8,128)(2,1)S(1)}, bf16[128,2048]{1,0:T(8,128)(2,1)S(1)}, u32[]{:S(2)}, u32[]{:S(2)}) collective-permute-start(bf16[128,2048]{1,0:T(8,128)(2,1)S(1)} %get-tuple-element.50), channel_id=1, source_target_pairs={{0,96},{32,0},{64,32},{96,64},{1,97},{33,1},{65,33},{97,65},{2,98}... | collective-permute-start | bytes 1572872 | tf_op jit(solution)/shard_map/ppermute | solution.py:118
  78.9 1.1 collective-permute-start.20
  80.1 0.0 collective-permute-done.3.refs_1_
  80.1 0.8 collective-permute-start.21
  80.9 0.0 collective-permute-done.4.refs_2_
  80.9 0.0 collective-permute-done.5.refs_3_
  80.9 8.8 %shard_map.66 = (bf16[128,2048]{1,0:T(8,128)(2,1)S(1)}, bf16[128,2048]{1,0:T(8,128)(2,1)S(1)}, bf16[128,2048]{1,0:T(8,128)(2,1)S(1)}, bf16[128,2048]{1,0:T(8,128)(2,1)S(1)}) custom-call(bf16[1,2048,768]{2,1,0:T(8,128)(2,1)} %gate_ref.3, bf16[1,2048,768]{2,1,0:T(8,128)(2,1)} %up_ref.3, bf16[1,768,2048]{2,1,0:T(8,128)(2,1)} %down_ref.3, ...), custom_call_target="tpu_custom_call" | custom-call | tf_op jit(solution)/shard_map/pallas_call | solution.py:103
  89.7 3.8 %collective-permute-start.6 = (bf16[128,2048]{1,0:T(8,128)(2,1)S(1)}, bf16[128,2048]{1,0:T(8,128)(2,1)S(1)}, u32[]{:S(2)}, u32[]{:S(2)}) collective-permute-start(bf16[128,2048]{1,0:T(8,128)(2,1)S(1)} %get-tuple-element.37), channel_id=1, source_target_pairs={{0,24},{8,0},{16,8},{24,16},{1,25},{9,1},{17,9},{25,17},{2,26},{10... | collective-permute-start | bytes 1572872 | tf_op jit(solution)/shard_map/ppermute | solution.py:118
  93.5 0.6 collective-permute-start.7
  94.0 6.7 %collective-permute-done.19.refs_1_ = bf16[128,2048]{1,0:T(8,128)(2,1)S(1)} collective-permute-done((bf16[128,2048]{1,0:T(8,128)(2,1)S(1)}, bf16[128,2048]{1,0:T(8,128)(2,1)S(1)}, u32[]{:S(2)}, u32[]{:S(2)}) %collective-permute-start.19) | collective-permute-done | bytes 524320 | tf_op jit(solution)/shard_map/ppermute | solution.py:118
  100.8 2.9 %collective-permute-start.8 = (bf16[128,2048]{1,0:T(8,128)(2,1)S(1)}, bf16[128,2048]{1,0:T(8,128)(2,1)S(1)}, u32[]{:S(2)}, u32[]{:S(2)}) collective-permute-start(bf16[128,2048]{1,0:T(8,128)(2,1)S(1)} %get-tuple-element.39), channel_id=1, source_target_pairs={{0,8},{8,16},{16,24},{24,0},{1,9},{9,17},{17,25},{25,1},{2,10},{10... | collective-permute-start | bytes 1572872 | tf_op jit(solution)/shard_map/ppermute | solution.py:118
  103.7 0.0 collective-permute-done.20.refs_2_
  103.7 0.8 collective-permute-done.21.refs_3_
  104.5 0.7 shard_map.70
  105.2 2.8 %collective-permute-start.24 = (bf16[64,2048]{1,0:T(8,128)(2,1)S(1)}, bf16[64,2048]{1,0:T(8,128)(2,1)S(1)}, u32[]{:S(2)}, u32[]{:S(2)}) collective-permute-start(bf16[64,2048]{1,0:T(8,128)(2,1)S(1)} %get-tuple-element.56), channel_id=1, source_target_pairs={{0,8},{8,16},{16,24},{24,0},{1,9},{9,17},{17,25},{25,1},{2,10},{10... | collective-permute-start | bytes 786440 | tf_op jit(solution)/shard_map/ppermute | solution.py:118
  108.0 3.0 %collective-permute-start.23 = (bf16[64,2048]{1,0:T(8,128)(2,1)S(1)}, bf16[64,2048]{1,0:T(8,128)(2,1)S(1)}, u32[]{:S(2)}, u32[]{:S(2)}) collective-permute-start(bf16[64,2048]{1,0:T(8,128)(2,1)S(1)} %get-tuple-element.55), channel_id=1, source_target_pairs={{0,16},{8,24},{16,0},{24,8},{1,17},{9,25},{17,1},{25,9},{2,18},{10... | collective-permute-start | bytes 786440 | tf_op jit(solution)/shard_map/ppermute | solution.py:118
  110.9 10.7 %collective-permute-done.6.refs_1_ = bf16[128,2048]{1,0:T(8,128)(2,1)S(1)} collective-permute-done((bf16[128,2048]{1,0:T(8,128)(2,1)S(1)}, bf16[128,2048]{1,0:T(8,128)(2,1)S(1)}, u32[]{:S(2)}, u32[]{:S(2)}) %collective-permute-start.6) | collective-permute-done | bytes 524320 | tf_op jit(solution)/shard_map/ppermute | solution.py:118
  121.7 3.8 %collective-permute-start.22 = (bf16[64,2048]{1,0:T(8,128)(2,1)S(1)}, bf16[64,2048]{1,0:T(8,128)(2,1)S(1)}, u32[]{:S(2)}, u32[]{:S(2)}) collective-permute-start(bf16[64,2048]{1,0:T(8,128)(2,1)S(1)} %get-tuple-element.54), channel_id=1, source_target_pairs={{0,24},{8,0},{16,8},{24,16},{1,25},{9,1},{17,9},{25,17},{2,26},{10... | collective-permute-start | bytes 786440 | tf_op jit(solution)/shard_map/ppermute | solution.py:118
  125.5 0.0 collective-permute-done.7.refs_2_
  125.5 0.0 collective-permute-done.8.refs_3_
  125.5 0.7 shard_map.67
  126.2 2.3 %collective-permute-start.11 = (bf16[64,2048]{1,0:T(8,128)(2,1)S(1)}, bf16[64,2048]{1,0:T(8,128)(2,1)S(1)}, u32[]{:S(2)}, u32[]{:S(2)}) collective-permute-start(bf16[64,2048]{1,0:T(8,128)(2,1)S(1)} %get-tuple-element.43), channel_id=1, source_target_pairs={{0,32},{32,64},{64,96},{96,0},{1,33},{33,65},{65,97},{97,1},{2,34}... | collective-permute-start | bytes 786440 | tf_op jit(solution)/shard_map/ppermute | solution.py:118
  128.5 1.6 %collective-permute-start.10 = (bf16[64,2048]{1,0:T(8,128)(2,1)S(1)}, bf16[64,2048]{1,0:T(8,128)(2,1)S(1)}, u32[]{:S(2)}, u32[]{:S(2)}) collective-permute-start(bf16[64,2048]{1,0:T(8,128)(2,1)S(1)} %get-tuple-element.42), channel_id=1, source_target_pairs={{0,64},{32,96},{64,0},{96,32},{1,65},{33,97},{65,1},{97,33},{2,66}... | collective-permute-start | bytes 786440 | tf_op jit(solution)/shard_map/ppermute | solution.py:118
  130.1 0.0 collective-permute-done.24
  130.1 1.2 collective-permute-start.9
  131.3 0.0 collective-permute-done.23
  131.3 0.0 collective-permute-done.22
  131.3 0.1 add_convert_fusion.1
  131.5 1.5 %collective-permute-start.25 = (bf16[64,2048]{1,0:T(8,128)(2,1)S(1)}, bf16[64,2048]{1,0:T(8,128)(2,1)S(1)}, u32[]{:S(2)}, u32[]{:S(2)}) collective-permute-start(bf16[64,2048]{1,0:T(8,128)(2,1)S(1)} %add_convert_fusion.1), channel_id=1, source_target_pairs={{0,128},{128,0},{1,129},{129,1},{2,130},{130,2},{3,131},{131,3},{4... | collective-permute-start | bytes 786440 | tf_op jit(solution)/shard_map/ppermute | solution.py:118
  132.9 0.9 collective-permute-done.11
  133.9 3.4 %collective-permute-done.10 = bf16[64,2048]{1,0:T(8,128)(2,1)S(1)} collective-permute-done((bf16[64,2048]{1,0:T(8,128)(2,1)S(1)}, bf16[64,2048]{1,0:T(8,128)(2,1)S(1)}, u32[]{:S(2)}, u32[]{:S(2)}) %collective-permute-start.10) | collective-permute-done | bytes 262176 | tf_op jit(solution)/shard_map/ppermute | solution.py:118
  137.3 0.3 collective-permute-done.9
  137.5 0.4 collective-permute-done.25
  137.9 0.9 add_convert_fusion
  (5 shorter events, 0.0 us)
Async XLA Ops:
  0.0 0.9 copy-start
  1.0 0.7 copy-start.1
  1.6 0.7 copy-start.2
  2.8 8.7 %collective-permute-start.12 = (bf16[64,2176]{1,0:T(8,128)(2,1)S(1)}, bf16[64,2176]{1,0:T(8,128)(2,1)S(1)}, u32[]{:S(2)}, u32[]{:S(2)}) collective-permute-start(bf16[64,2176]{1,0:T(8,128)(2,1)S(1)} %shard_map.64.refs_0_), channel_id=1, source_target_pairs={{0,128},{128,0},{1,129},{129,1},{2,130},{130,2},{3,131},{131,3},{4... | collective-permute-start | bytes 835592 | tf_op jit(solution)/shard_map/ppermute | solution.py:118
  11.5 9.8 %collective-permute-start.13 = (bf16[64,2176]{1,0:T(8,128)(2,1)S(1)}, bf16[64,2176]{1,0:T(8,128)(2,1)S(1)}, u32[]{:S(2)}, u32[]{:S(2)}) collective-permute-start(bf16[64,2176]{1,0:T(8,128)(2,1)S(1)} %collective-permute-done.12.refs_0_), channel_id=1, source_target_pairs={{0,8},{8,16},{16,24},{24,0},{1,9},{9,17},{17,25},{25,1},{2,10},{10... | collective-permute-start | bytes 835592 | tf_op jit(solution)/shard_map/ppermute | solution.py:118
  13.0 14.4 %collective-permute-start.14 = (bf16[64,2176]{1,0:T(8,128)(2,1)S(1)}, bf16[64,2176]{1,0:T(8,128)(2,1)S(1)}, u32[]{:S(2)}, u32[]{:S(2)}) collective-permute-start(bf16[64,2176]{1,0:T(8,128)(2,1)S(1)} %collective-permute-done.12.refs_0_), channel_id=1, source_target_pairs={{0,16},{8,24},{16,0},{24,8},{1,17},{9,25},{17,1},{25,9},{2,18},{10... | collective-permute-start | bytes 835592 | tf_op jit(solution)/shard_map/ppermute | solution.py:118
  15.7 11.7 %collective-permute-start.15 = (bf16[64,2176]{1,0:T(8,128)(2,1)S(1)}, bf16[64,2176]{1,0:T(8,128)(2,1)S(1)}, u32[]{:S(2)}, u32[]{:S(2)}) collective-permute-start(bf16[64,2176]{1,0:T(8,128)(2,1)S(1)} %collective-permute-done.12.refs_0_), channel_id=1, source_target_pairs={{0,24},{8,0},{16,8},{24,16},{1,25},{9,1},{17,9},{25,17},{2,26},{10... | collective-permute-start | bytes 835592 | tf_op jit(solution)/shard_map/ppermute | solution.py:118
  17.1 19.1 %collective-permute-start = (bf16[64,2176]{1,0:T(8,128)(2,1)S(1)}, bf16[64,2176]{1,0:T(8,128)(2,1)S(1)}, u32[]{:S(2)}, u32[]{:S(2)}) collective-permute-start(bf16[64,2176]{1,0:T(8,128)(2,1)S(1)} %shard_map.64.refs_0_), channel_id=1, source_target_pairs={{0,32},{32,64},{64,96},{96,0},{1,33},{33,65},{65,97},{97,1},{2,34}... | collective-permute-start | bytes 835592 | tf_op jit(solution)/shard_map/ppermute | solution.py:118
  30.0 28.7 %collective-permute-start.16 = (bf16[128,2048]{1,0:T(8,128)(2,1)}, bf16[128,2048]{1,0:T(8,128)(2,1)S(1)}, u32[]{:S(2)}, u32[]{:S(2)}) collective-permute-start(bf16[128,2048]{1,0:T(8,128)(2,1)} %get-tuple-element.46), channel_id=1, source_target_pairs={{0,32},{32,64},{64,96},{96,0},{1,33},{33,65},{65,97},{97,1},{2,34}... | collective-permute-start | bytes 1572872 | tf_op jit(solution)/shard_map/ppermute | solution.py:118
  31.6 21.8 %collective-permute-start.1 = (bf16[64,2176]{1,0:T(8,128)(2,1)S(1)}, bf16[64,2176]{1,0:T(8,128)(2,1)S(1)}, u32[]{:S(2)}, u32[]{:S(2)}) collective-permute-start(bf16[64,2176]{1,0:T(8,128)(2,1)S(1)} %shard_map.64.refs_0_), channel_id=1, source_target_pairs={{0,64},{32,96},{64,0},{96,32},{1,65},{33,97},{65,1},{97,33},{2,66}... | collective-permute-start | bytes 835592 | tf_op jit(solution)/shard_map/ppermute | solution.py:118
  34.5 19.1 %collective-permute-start.2 = (bf16[64,2176]{1,0:T(8,128)(2,1)S(1)}, bf16[64,2176]{1,0:T(8,128)(2,1)S(1)}, u32[]{:S(2)}, u32[]{:S(2)}) collective-permute-start(bf16[64,2176]{1,0:T(8,128)(2,1)S(1)} %shard_map.64.refs_0_), channel_id=1, source_target_pairs={{0,96},{32,0},{64,32},{96,64},{1,97},{33,1},{65,33},{97,65},{2,98}... | collective-permute-start | bytes 835592 | tf_op jit(solution)/shard_map/ppermute | solution.py:118
  35.8 26.4 %collective-permute-start.17 = (bf16[128,2048]{1,0:T(8,128)(2,1)}, bf16[128,2048]{1,0:T(8,128)(2,1)S(1)}, u32[]{:S(2)}, u32[]{:S(2)}) collective-permute-start(bf16[128,2048]{1,0:T(8,128)(2,1)} %get-tuple-element.47), channel_id=1, source_target_pairs={{0,64},{32,96},{64,0},{96,32},{1,65},{33,97},{65,1},{97,33},{2,66}... | collective-permute-start | bytes 1572872 | tf_op jit(solution)/shard_map/ppermute | solution.py:118
  36.2 31.2 %collective-permute-start.18 = (bf16[128,2048]{1,0:T(8,128)(2,1)}, bf16[128,2048]{1,0:T(8,128)(2,1)S(1)}, u32[]{:S(2)}, u32[]{:S(2)}) collective-permute-start(bf16[128,2048]{1,0:T(8,128)(2,1)} %get-tuple-element.48), channel_id=1, source_target_pairs={{0,96},{32,0},{64,32},{96,64},{1,97},{33,1},{65,33},{97,65},{2,98}... | collective-permute-start | bytes 1572872 | tf_op jit(solution)/shard_map/ppermute | solution.py:118
  55.1 24.9 %collective-permute-start.3 = (bf16[128,2048]{1,0:T(8,128)(2,1)S(1)}, bf16[128,2048]{1,0:T(8,128)(2,1)S(1)}, u32[]{:S(2)}, u32[]{:S(2)}) collective-permute-start(bf16[128,2048]{1,0:T(8,128)(2,1)S(1)} %get-tuple-element.33), channel_id=1, source_target_pairs={{0,8},{8,16},{16,24},{24,0},{1,9},{9,17},{17,25},{25,1},{2,10},{10... | collective-permute-start | bytes 1572872 | tf_op jit(solution)/shard_map/ppermute | solution.py:118
  56.4 24.5 %collective-permute-start.4 = (bf16[128,2048]{1,0:T(8,128)(2,1)S(1)}, bf16[128,2048]{1,0:T(8,128)(2,1)S(1)}, u32[]{:S(2)}, u32[]{:S(2)}) collective-permute-start(bf16[128,2048]{1,0:T(8,128)(2,1)S(1)} %get-tuple-element.34), channel_id=1, source_target_pairs={{0,16},{8,24},{16,0},{24,8},{1,17},{9,25},{17,1},{25,9},{2,18},{10... | collective-permute-start | bytes 1572872 | tf_op jit(solution)/shard_map/ppermute | solution.py:118
  58.8 22.1 %collective-permute-start.5 = (bf16[128,2048]{1,0:T(8,128)(2,1)S(1)}, bf16[128,2048]{1,0:T(8,128)(2,1)S(1)}, u32[]{:S(2)}, u32[]{:S(2)}) collective-permute-start(bf16[128,2048]{1,0:T(8,128)(2,1)S(1)} %get-tuple-element.35), channel_id=1, source_target_pairs={{0,24},{8,0},{16,8},{24,16},{1,25},{9,1},{17,9},{25,17},{2,26},{10... | collective-permute-start | bytes 1572872 | tf_op jit(solution)/shard_map/ppermute | solution.py:118
  76.2 24.6 %collective-permute-start.19 = (bf16[128,2048]{1,0:T(8,128)(2,1)S(1)}, bf16[128,2048]{1,0:T(8,128)(2,1)S(1)}, u32[]{:S(2)}, u32[]{:S(2)}) collective-permute-start(bf16[128,2048]{1,0:T(8,128)(2,1)S(1)} %get-tuple-element.50), channel_id=1, source_target_pairs={{0,96},{32,0},{64,32},{96,64},{1,97},{33,1},{65,33},{97,65},{2,98}... | collective-permute-start | bytes 1572872 | tf_op jit(solution)/shard_map/ppermute | solution.py:118
  78.9 24.8 %collective-permute-start.20 = (bf16[128,2048]{1,0:T(8,128)(2,1)S(1)}, bf16[128,2048]{1,0:T(8,128)(2,1)S(1)}, u32[]{:S(2)}, u32[]{:S(2)}) collective-permute-start(bf16[128,2048]{1,0:T(8,128)(2,1)S(1)} %get-tuple-element.51), channel_id=1, source_target_pairs={{0,64},{32,96},{64,0},{96,32},{1,65},{33,97},{65,1},{97,33},{2,66}... | collective-permute-start | bytes 1572872 | tf_op jit(solution)/shard_map/ppermute | solution.py:118
  80.1 24.4 %collective-permute-start.21 = (bf16[128,2048]{1,0:T(8,128)(2,1)S(1)}, bf16[128,2048]{1,0:T(8,128)(2,1)S(1)}, u32[]{:S(2)}, u32[]{:S(2)}) collective-permute-start(bf16[128,2048]{1,0:T(8,128)(2,1)S(1)} %get-tuple-element.52), channel_id=1, source_target_pairs={{0,32},{32,64},{64,96},{96,0},{1,33},{33,65},{65,97},{97,1},{2,34}... | collective-permute-start | bytes 1572872 | tf_op jit(solution)/shard_map/ppermute | solution.py:118
  89.7 31.9 %collective-permute-start.6 = (bf16[128,2048]{1,0:T(8,128)(2,1)S(1)}, bf16[128,2048]{1,0:T(8,128)(2,1)S(1)}, u32[]{:S(2)}, u32[]{:S(2)}) collective-permute-start(bf16[128,2048]{1,0:T(8,128)(2,1)S(1)} %get-tuple-element.37), channel_id=1, source_target_pairs={{0,24},{8,0},{16,8},{24,16},{1,25},{9,1},{17,9},{25,17},{2,26},{10... | collective-permute-start | bytes 1572872 | tf_op jit(solution)/shard_map/ppermute | solution.py:118
  93.5 32.0 %collective-permute-start.7 = (bf16[128,2048]{1,0:T(8,128)(2,1)S(1)}, bf16[128,2048]{1,0:T(8,128)(2,1)S(1)}, u32[]{:S(2)}, u32[]{:S(2)}) collective-permute-start(bf16[128,2048]{1,0:T(8,128)(2,1)S(1)} %get-tuple-element.38), channel_id=1, source_target_pairs={{0,16},{8,24},{16,0},{24,8},{1,17},{9,25},{17,1},{25,9},{2,18},{10... | collective-permute-start | bytes 1572872 | tf_op jit(solution)/shard_map/ppermute | solution.py:118
  100.8 24.7 %collective-permute-start.8 = (bf16[128,2048]{1,0:T(8,128)(2,1)S(1)}, bf16[128,2048]{1,0:T(8,128)(2,1)S(1)}, u32[]{:S(2)}, u32[]{:S(2)}) collective-permute-start(bf16[128,2048]{1,0:T(8,128)(2,1)S(1)} %get-tuple-element.39), channel_id=1, source_target_pairs={{0,8},{8,16},{16,24},{24,0},{1,9},{9,17},{17,25},{25,1},{2,10},{10... | collective-permute-start | bytes 1572872 | tf_op jit(solution)/shard_map/ppermute | solution.py:118
  105.2 24.9 %collective-permute-start.24 = (bf16[64,2048]{1,0:T(8,128)(2,1)S(1)}, bf16[64,2048]{1,0:T(8,128)(2,1)S(1)}, u32[]{:S(2)}, u32[]{:S(2)}) collective-permute-start(bf16[64,2048]{1,0:T(8,128)(2,1)S(1)} %get-tuple-element.56), channel_id=1, source_target_pairs={{0,8},{8,16},{16,24},{24,0},{1,9},{9,17},{17,25},{25,1},{2,10},{10... | collective-permute-start | bytes 786440 | tf_op jit(solution)/shard_map/ppermute | solution.py:118
  108.0 23.3 %collective-permute-start.23 = (bf16[64,2048]{1,0:T(8,128)(2,1)S(1)}, bf16[64,2048]{1,0:T(8,128)(2,1)S(1)}, u32[]{:S(2)}, u32[]{:S(2)}) collective-permute-start(bf16[64,2048]{1,0:T(8,128)(2,1)S(1)} %get-tuple-element.55), channel_id=1, source_target_pairs={{0,16},{8,24},{16,0},{24,8},{1,17},{9,25},{17,1},{25,9},{2,18},{10... | collective-permute-start | bytes 786440 | tf_op jit(solution)/shard_map/ppermute | solution.py:118
  121.7 9.7 %collective-permute-start.22 = (bf16[64,2048]{1,0:T(8,128)(2,1)S(1)}, bf16[64,2048]{1,0:T(8,128)(2,1)S(1)}, u32[]{:S(2)}, u32[]{:S(2)}) collective-permute-start(bf16[64,2048]{1,0:T(8,128)(2,1)S(1)} %get-tuple-element.54), channel_id=1, source_target_pairs={{0,24},{8,0},{16,8},{24,16},{1,25},{9,1},{17,9},{25,17},{2,26},{10... | collective-permute-start | bytes 786440 | tf_op jit(solution)/shard_map/ppermute | solution.py:118
  126.2 7.7 %collective-permute-start.11 = (bf16[64,2048]{1,0:T(8,128)(2,1)S(1)}, bf16[64,2048]{1,0:T(8,128)(2,1)S(1)}, u32[]{:S(2)}, u32[]{:S(2)}) collective-permute-start(bf16[64,2048]{1,0:T(8,128)(2,1)S(1)} %get-tuple-element.43), channel_id=1, source_target_pairs={{0,32},{32,64},{64,96},{96,0},{1,33},{33,65},{65,97},{97,1},{2,34}... | collective-permute-start | bytes 786440 | tf_op jit(solution)/shard_map/ppermute | solution.py:118
  128.5 8.7 %collective-permute-start.10 = (bf16[64,2048]{1,0:T(8,128)(2,1)S(1)}, bf16[64,2048]{1,0:T(8,128)(2,1)S(1)}, u32[]{:S(2)}, u32[]{:S(2)}) collective-permute-start(bf16[64,2048]{1,0:T(8,128)(2,1)S(1)} %get-tuple-element.42), channel_id=1, source_target_pairs={{0,64},{32,96},{64,0},{96,32},{1,65},{33,97},{65,1},{97,33},{2,66}... | collective-permute-start | bytes 786440 | tf_op jit(solution)/shard_map/ppermute | solution.py:118
  130.1 7.4 %collective-permute-start.9 = (bf16[64,2048]{1,0:T(8,128)(2,1)S(1)}, bf16[64,2048]{1,0:T(8,128)(2,1)S(1)}, u32[]{:S(2)}, u32[]{:S(2)}) collective-permute-start(bf16[64,2048]{1,0:T(8,128)(2,1)S(1)} %get-tuple-element.41), channel_id=1, source_target_pairs={{0,96},{32,0},{64,32},{96,64},{1,97},{33,1},{65,33},{97,65},{2,98}... | collective-permute-start | bytes 786440 | tf_op jit(solution)/shard_map/ppermute | solution.py:118
  131.5 6.5 %collective-permute-start.25 = (bf16[64,2048]{1,0:T(8,128)(2,1)S(1)}, bf16[64,2048]{1,0:T(8,128)(2,1)S(1)}, u32[]{:S(2)}, u32[]{:S(2)}) collective-permute-start(bf16[64,2048]{1,0:T(8,128)(2,1)S(1)} %add_convert_fusion.1), channel_id=1, source_target_pairs={{0,128},{128,0},{1,129},{129,1},{2,130},{130,2},{3,131},{131,3},{4... | collective-permute-start | bytes 786440 | tf_op jit(solution)/shard_map/ppermute | solution.py:118
where the time goes:
time: 139 us
  waiting for transfers between devices  59.7 us (43%)
  starting transfers between devices  52 us (37%)
  Pallas kernels  23.6 us (17%)
  local copies, waits for them, and re-layouts  2.32 us (2%)
    ppermute x26, waiting for transfers between devices, shift(): lax.ppermute(value, axis, [(i, (i + by) % count) for i in range(count)])  59.7 us
    ppermute x26, starting transfers between devices, shift(): lax.ppermute(value, axis, [(i, (i + by) % count) for i in range(count)])  52 us
    pallas_call x7, Pallas kernels, call(): pl.pallas_call(kernel, out_shape=shapes, in_specs=[pl.BlockSpec(memory_sp...  23.6 us
  transfers between devices with their start and end apart: 26, of which 14 were waited for; matrix products, arithmetic and copies ran while one was open for 0% of the time, Pallas kernels for 17%

commit v1 on v0

--- a/solution.py
+++ b/solution.py
@@ -15,21 +15,14 @@
 SLOTS = SIDE * CAP
 NONE = 255.0
 VMEM = pl.BlockSpec(memory_space=pltpu.VMEM)
-PARAMS = pltpu.CompilerParams(vmem_limit_bytes=48 * 1024 * 1024)
 
 
-def prep_kernel(tok_hbm, ids_hbm, prob_hbm, out_ref, ids_ref, prob_ref, sems):
-    rows, features = tok_hbm.shape
-    top = ids_hbm.shape[0]
-    pairs = ((ids_hbm, ids_ref), (prob_hbm, prob_ref), (tok_hbm, out_ref.at[:, :features]))
-    copies = [pltpu.make_async_copy(a, b, sems.at[i]) for i, (a, b) in enumerate(pairs)]
-    for copy in copies:
-        copy.start()
-    copies[0].wait()
-    copies[1].wait()
-    prob = prob_ref[...]
-    weight = (prob / jnp.sum(prob, axis=0, keepdims=True)).T
-    ids = ids_ref[...].astype(F32).T
+def prep_kernel(tok_ref, table_ref, out_ref):
+    rows, features = tok_ref.shape
+    top = table_ref.shape[0] // 2
+    out_ref[:, :features] = tok_ref[...]
+    table = table_ref[...].T
+    ids, weight = table[:, :top], table[:, top:]
     lane = lax.broadcasted_iota(jnp.int32, (rows, META), 1)
     expert = (lane % EXPERTS).astype(F32)
     named = jnp.zeros((rows, META), F32)
@@ -47,7 +40,6 @@
     part = lane // EXPERTS
     meta = jnp.where(part == 0, slot, jnp.where(part == 1, high, value - high))
     out_ref[:, features:] = meta.astype(BF16)
-    copies[2].wait()
 
 
 def pack_kernel(owner_ref, *refs):
@@ -99,14 +91,14 @@
             outs[d][:, cols] = out[d * height : (d + 1) * height, :]
 
 
-def call(kernel, shapes, *args, scratch=(), space=pltpu.VMEM):
+def call(kernel, shapes, *args, scratch=(), limit=12):
     return pl.pallas_call(
         kernel,
         out_shape=shapes,
-        in_specs=[pl.BlockSpec(memory_space=space)] * len(args),
+        in_specs=[VMEM] * len(args),
         out_specs=jax.tree.map(lambda _: VMEM, shapes),
         scratch_shapes=scratch,
-        compiler_params=PARAMS,
+        compiler_params=pltpu.CompilerParams(vmem_limit_bytes=limit * 1024 * 1024),
     )(*args)
 
 
@@ -127,7 +119,6 @@
 
 def shards(tokens, expert_ids, gate_probs, w_gate, w_up, w_down):
     count, features = tokens.shape
-    top = expert_ids.shape[1]
     inner = w_gate.shape[2]
     z, y, x = (lax.axis_index(n) for n in "zyx")
     step = (jnp.arange(SLOTS, dtype=jnp.int32) // CAP)[None, :]
@@ -135,11 +126,9 @@
     owners = (base + y * SIDE + (x + step) % SIDE, base + (y + step) % SIDE * SIDE + x)
     shape = jax.ShapeDtypeStruct
 
-    mine = call(
-        prep_kernel, shape((count, features + META), BF16), tokens, expert_ids.T, gate_probs.T,
-        space=pltpu.HBM,
-        scratch=[pltpu.VMEM((top, count), jnp.int32), pltpu.VMEM((top, count), F32), pltpu.SemaphoreType.DMA((3,))],
-    )
+    weights = gate_probs / jnp.sum(gate_probs, axis=1, keepdims=True)
+    table = jnp.concatenate([expert_ids.astype(F32), weights], axis=1).T
+    mine = call(prep_kernel, shape((count, features + META), BF16), tokens, table, limit=8)
     theirs = shift(mine, "z", 1)
     pack_shapes = [shape((SLOTS, features), BF16)] * SIDE + [shape((SIDE, count, 2 * SLOTS), BF16)]
     unpack_shapes = [shape((count, features), BF16)] * SIDE
@@ -152,7 +141,7 @@
         gathered = shift_all([block] * SIDE, first, 1)
         *packed, weights = call(pack_kernel, pack_shapes, owner, *gathered)
         arrived = shift_all(packed, last, 1)
-        served = call(ffn_kernel, ffn_shapes, w_gate, w_up, w_down, *arrived, scratch=scratch)
+        served = call(ffn_kernel, ffn_shapes, w_gate, w_up, w_down, *arrived, scratch=scratch, limit=24)
         back = shift_all(served, last, -1)
         summed = call(unpack_kernel, unpack_shapes, weights, *back)
         partial.append(sum(p.astype(F32) for p in shift_all(summed, first, -1)))

time: 139 us -> 140 us (level)
  the two profiles are of different devices: /device:TPU:64 before, /device:TPU:88 now
where the time goes in v1:
time: 140 us
  waiting for transfers between devices  69.1 us (49%)
  starting transfers between devices  44.7 us (32%)
  Pallas kernels  16.1 us (12%)
  local copies, waits for them, and re-layouts  6.63 us (5%)
  other arithmetic  3.13 us (2%)
    ppermute x26, waiting for transfers between devices, shift(): lax.ppermute(value, axis, [(i, (i + by) % count) for i in range(count)])  69.1 us
    ppermute x26, starting transfers between devices, shift(): lax.ppermute(value, axis, [(i, (i + by) % count) for i in range(count)])  44.7 us
    pallas_call x7, Pallas kernels, call(): pl.pallas_call(kernel, out_shape=shapes, in_specs=[VMEM] * len(args), out...  16.1 us
    unnamed x14, local copies, waits for them, and re-layouts  6.63 us
  transfers between devices with their start and end apart: 26, of which 11 were waited for; matrix products, arithmetic and copies ran while one was open for 0% of the time, Pallas kernels for 11%

profile of v1, /device:TPU:88, one launch (start us, length us, event | category | flops | bytes accessed | tf_op | source)
XLA Modules:
  0.0 139.7 jit_solution(15894197082288183393)
XLA Ops:
  0.0 0.7 reduce_sum.9
  0.7 0.7 broadcast_divide_fusion
  1.4 0.7 convert_element_type.36
  2.1 0.9 copy-done.6
  3.0 0.4 shard_map.64.refs_0_
  3.4 1.9 %collective-permute-start.12 = (bf16[64,2176]{1,0:T(8,128)(2,1)S(1)}, bf16[64,2176]{1,0:T(8,128)(2,1)S(1)}, u32[]{:S(2)}, u32[]{:S(2)}) collective-permute-start(bf16[64,2176]{1,0:T(8,128)(2,1)S(1)} %shard_map.64.refs_0_), channel_id=1, source_target_pairs={{0,128},{128,0},{1,129},{129,1},{2,130},{130,2},{3,131},{131,3},{4... | collective-permute-start | bytes 835592 | tf_op jit(solution)/shard_map/ppermute | solution.py:110
  5.4 6.7 %collective-permute-done.12.refs_0_ = bf16[64,2176]{1,0:T(8,128)(2,1)S(1)} collective-permute-done((bf16[64,2176]{1,0:T(8,128)(2,1)S(1)}, bf16[64,2176]{1,0:T(8,128)(2,1)S(1)}, u32[]{:S(2)}, u32[]{:S(2)}) %collective-permute-start.12) | collective-permute-done | bytes 278560 | tf_op jit(solution)/shard_map/ppermute | solution.py:110
  12.1 1.5 %collective-permute-start.13 = (bf16[64,2176]{1,0:T(8,128)(2,1)S(1)}, bf16[64,2176]{1,0:T(8,128)(2,1)S(1)}, u32[]{:S(2)}, u32[]{:S(2)}) collective-permute-start(bf16[64,2176]{1,0:T(8,128)(2,1)S(1)} %collective-permute-done.12.refs_0_), channel_id=1, source_target_pairs={{0,8},{8,16},{16,24},{24,0},{1,9},{9,17},{17,25},{25,1},{2,10},{10... | collective-permute-start | bytes 835592 | tf_op jit(solution)/shard_map/ppermute | solution.py:110
  13.5 2.7 %collective-permute-start.14 = (bf16[64,2176]{1,0:T(8,128)(2,1)S(1)}, bf16[64,2176]{1,0:T(8,128)(2,1)S(1)}, u32[]{:S(2)}, u32[]{:S(2)}) collective-permute-start(bf16[64,2176]{1,0:T(8,128)(2,1)S(1)} %collective-permute-done.12.refs_0_), channel_id=1, source_target_pairs={{0,16},{8,24},{16,0},{24,8},{1,17},{9,25},{17,1},{25,9},{2,18},{10... | collective-permute-start | bytes 835592 | tf_op jit(solution)/shard_map/ppermute | solution.py:110
  16.3 1.4 %collective-permute-start.15 = (bf16[64,2176]{1,0:T(8,128)(2,1)S(1)}, bf16[64,2176]{1,0:T(8,128)(2,1)S(1)}, u32[]{:S(2)}, u32[]{:S(2)}) collective-permute-start(bf16[64,2176]{1,0:T(8,128)(2,1)S(1)} %collective-permute-done.12.refs_0_), channel_id=1, source_target_pairs={{0,24},{8,0},{16,8},{24,16},{1,25},{9,1},{17,9},{25,17},{2,26},{10... | collective-permute-start | bytes 835592 | tf_op jit(solution)/shard_map/ppermute | solution.py:110
  17.7 0.2 collective-permute-start
  18.0 3.9 %collective-permute-done.13.refs_1_ = bf16[64,2176]{1,0:T(8,128)(2,1)S(1)} collective-permute-done((bf16[64,2176]{1,0:T(8,128)(2,1)S(1)}, bf16[64,2176]{1,0:T(8,128)(2,1)S(1)}, u32[]{:S(2)}, u32[]{:S(2)}) %collective-permute-start.13) | collective-permute-done | bytes 278560 | tf_op jit(solution)/shard_map/ppermute | solution.py:110
  21.8 6.1 %collective-permute-done.14.refs_2_ = bf16[64,2176]{1,0:T(8,128)(2,1)S(1)} collective-permute-done((bf16[64,2176]{1,0:T(8,128)(2,1)S(1)}, bf16[64,2176]{1,0:T(8,128)(2,1)S(1)}, u32[]{:S(2)}, u32[]{:S(2)}) %collective-permute-start.14) | collective-permute-done | bytes 278560 | tf_op jit(solution)/shard_map/ppermute | solution.py:110
  27.9 0.0 collective-permute-done.15.refs_3_
  27.9 2.7 %shard_map.68 = (bf16[128,2048]{1,0:T(8,128)(2,1)S(1)}, bf16[128,2048]{1,0:T(8,128)(2,1)}, bf16[128,2048]{1,0:T(8,128)(2,1)}, bf16[128,2048]{1,0:T(8,128)(2,1)}, bf16[4,64,256]{2,1,0:T(8,128)(2,1)S(1)}) custom-call(s32[1,128]{1,0:T(1,128)S(1)} %fusion.3.owner_ref, bf16[64,2176]{1,0:T(8,128)(2,1)S(1)} %collective-permute-done.12.refs_0_, ...), custom_call_target="tpu_custom_call" | custom-call | tf_op jit(solution)/shard_map/pallas_call | solution.py:95
  30.6 0.2 collective-permute-start.16
  30.8 2.6 %collective-permute-start.1 = (bf16[64,2176]{1,0:T(8,128)(2,1)S(1)}, bf16[64,2176]{1,0:T(8,128)(2,1)S(1)}, u32[]{:S(2)}, u32[]{:S(2)}) collective-permute-start(bf16[64,2176]{1,0:T(8,128)(2,1)S(1)} %shard_map.64.refs_0_), channel_id=1, source_target_pairs={{0,64},{32,96},{64,0},{96,32},{1,65},{33,97},{65,1},{97,33},{2,66}... | collective-permute-start | bytes 835592 | tf_op jit(solution)/shard_map/ppermute | solution.py:110
  33.4 0.0 collective-permute-start.2
  33.4 3.3 %collective-permute-start.17 = (bf16[128,2048]{1,0:T(8,128)(2,1)}, bf16[128,2048]{1,0:T(8,128)(2,1)S(1)}, u32[]{:S(2)}, u32[]{:S(2)}) collective-permute-start(bf16[128,2048]{1,0:T(8,128)(2,1)} %get-tuple-element.47), channel_id=1, source_target_pairs={{0,64},{32,96},{64,0},{96,32},{1,65},{33,97},{65,1},{97,33},{2,66}... | collective-permute-start | bytes 1572872 | tf_op jit(solution)/shard_map/ppermute | solution.py:110
  36.8 0.0 collective-permute-done.refs_1_
  36.8 0.7 collective-permute-start.18
  37.5 4.3 %collective-permute-done.1.refs_2_ = bf16[64,2176]{1,0:T(8,128)(2,1)S(1)} collective-permute-done((bf16[64,2176]{1,0:T(8,128)(2,1)S(1)}, bf16[64,2176]{1,0:T(8,128)(2,1)S(1)}, u32[]{:S(2)}, u32[]{:S(2)}) %collective-permute-start.1) | collective-permute-done | bytes 278560 | tf_op jit(solution)/shard_map/ppermute | solution.py:110
  41.9 13.5 %collective-permute-done.2.refs_3_ = bf16[64,2176]{1,0:T(8,128)(2,1)S(1)} collective-permute-done((bf16[64,2176]{1,0:T(8,128)(2,1)S(1)}, bf16[64,2176]{1,0:T(8,128)(2,1)S(1)}, u32[]{:S(2)}, u32[]{:S(2)}) %collective-permute-start.2) | collective-permute-done | bytes 278560 | tf_op jit(solution)/shard_map/ppermute | solution.py:110
  55.4 1.5 %shard_map.65 = (bf16[128,2048]{1,0:T(8,128)(2,1)S(1)}, bf16[128,2048]{1,0:T(8,128)(2,1)S(1)}, bf16[128,2048]{1,0:T(8,128)(2,1)S(1)}, bf16[128,2048]{1,0:T(8,128)(2,1)S(1)}, bf16[4,64,256]{2,1,0:T(8,128)(2,1)S(1)}) custom-call(s32[1,128]{1,0:T(1,128)S(1)} %fusion.owner_ref, bf16[64,2176]{1,0:T(8,128)(2,1)S(1)} %shard_map.64.refs_0_, ...), custom_call_target="tpu_custom_call" | custom-call | tf_op jit(solution)/shard_map/pallas_call | solution.py:95
  56.9 0.1 collective-permute-start.3
  57.0 2.8 %collective-permute-start.4 = (bf16[128,2048]{1,0:T(8,128)(2,1)S(1)}, bf16[128,2048]{1,0:T(8,128)(2,1)S(1)}, u32[]{:S(2)}, u32[]{:S(2)}) collective-permute-start(bf16[128,2048]{1,0:T(8,128)(2,1)S(1)} %get-tuple-element.34), channel_id=1, source_target_pairs={{0,16},{8,24},{16,0},{24,8},{1,17},{9,25},{17,1},{25,9},{2,18},{10... | collective-permute-start | bytes 1572872 | tf_op jit(solution)/shard_map/ppermute | solution.py:110
  59.7 0.0 collective-permute-done.16.refs_1_
  59.7 2.5 %collective-permute-start.5 = (bf16[128,2048]{1,0:T(8,128)(2,1)S(1)}, bf16[128,2048]{1,0:T(8,128)(2,1)S(1)}, u32[]{:S(2)}, u32[]{:S(2)}) collective-permute-start(bf16[128,2048]{1,0:T(8,128)(2,1)S(1)} %get-tuple-element.35), channel_id=1, source_target_pairs={{0,24},{8,0},{16,8},{24,16},{1,25},{9,1},{17,9},{25,17},{2,26},{10... | collective-permute-start | bytes 1572872 | tf_op jit(solution)/shard_map/ppermute | solution.py:110
  62.3 0.0 collective-permute-done.17.refs_2_
  62.3 5.4 %collective-permute-done.18.refs_3_ = bf16[128,2048]{1,0:T(8,128)(2,1)S(1)} collective-permute-done((bf16[128,2048]{1,0:T(8,128)(2,1)}, bf16[128,2048]{1,0:T(8,128)(2,1)S(1)}, u32[]{:S(2)}, u32[]{:S(2)}) %collective-permute-start.18) | collective-permute-done | bytes 524320 | tf_op jit(solution)/shard_map/ppermute | solution.py:110
  67.6 1.9 %copy-done = bf16[1,2048,768]{2,1,0:T(8,128)(2,1)S(1)} copy-done((bf16[1,2048,768]{2,1,0:T(8,128)(2,1)S(1)}, bf16[1,2048,768]{2,1,0:T(8,128)(2,1)}, u32[]{:S(2)}) %copy-start) | copy-done | bytes 3145752
  69.5 1.9 %copy-done.2 = bf16[1,2048,768]{2,1,0:T(8,128)(2,1)S(1)} copy-done((bf16[1,2048,768]{2,1,0:T(8,128)(2,1)S(1)}, bf16[1,2048,768]{2,1,0:T(8,128)(2,1)}, u32[]{:S(2)}) %copy-start.2) | copy-done | bytes 3145752
  71.4 1.9 %copy-done.4 = bf16[1,768,2048]{2,1,0:T(8,128)(2,1)S(1)} copy-done((bf16[1,768,2048]{2,1,0:T(8,128)(2,1)S(1)}, bf16[1,768,2048]{2,1,0:T(8,128)(2,1)}, u32[]{:S(2)}) %copy-start.4) | copy-done | bytes 3145752
  73.3 5.0 %shard_map.69 = (bf16[128,2048]{1,0:T(8,128)(2,1)S(1)}, bf16[128,2048]{1,0:T(8,128)(2,1)S(1)}, bf16[128,2048]{1,0:T(8,128)(2,1)S(1)}, bf16[128,2048]{1,0:T(8,128)(2,1)S(1)}) custom-call(bf16[1,2048,768]{2,1,0:T(8,128)(2,1)S(1)} %copy-done, bf16[1,2048,768]{2,1,0:T(8,128)(2,1)S(1)} %copy-done.2, bf16[1,768,2048]{2,1,0:T(8,128)(2,1)S(1)} %copy-done.4, ...), custom_call_target="tpu_custom_call" | custom-call | tf_op jit(solution)/shard_map/pallas_call | solution.py:95
  78.3 1.2 collective-permute-start.19
  79.5 0.9 collective-permute-start.20
  80.4 0.0 collective-permute-done.3.refs_1_
  80.4 2.4 %collective-permute-start.21 = (bf16[128,2048]{1,0:T(8,128)(2,1)S(1)}, bf16[128,2048]{1,0:T(8,128)(2,1)S(1)}, u32[]{:S(2)}, u32[]{:S(2)}) collective-permute-start(bf16[128,2048]{1,0:T(8,128)(2,1)S(1)} %get-tuple-element.52), channel_id=1, source_target_pairs={{0,32},{32,64},{64,96},{96,0},{1,33},{33,65},{65,97},{97,1},{2,34}... | collective-permute-start | bytes 1572872 | tf_op jit(solution)/shard_map/ppermute | solution.py:110
  82.8 0.0 collective-permute-done.4.refs_2_
  82.8 0.0 collective-permute-done.5.refs_3_
  82.8 5.0 %shard_map.66 = (bf16[128,2048]{1,0:T(8,128)(2,1)S(1)}, bf16[128,2048]{1,0:T(8,128)(2,1)S(1)}, bf16[128,2048]{1,0:T(8,128)(2,1)S(1)}, bf16[128,2048]{1,0:T(8,128)(2,1)S(1)}) custom-call(bf16[1,2048,768]{2,1,0:T(8,128)(2,1)S(1)} %copy-done.1, bf16[1,2048,768]{2,1,0:T(8,128)(2,1)S(1)} %copy-done.3, bf16[1,768,2048]{2,1,0:T(8,128)(2,1)S(1)} %copy-done.5, ...), custom_call_target="tpu_custom_call" | custom-call | tf_op jit(solution)/shard_map/pallas_call | solution.py:95
  87.9 3.8 %collective-permute-start.6 = (bf16[128,2048]{1,0:T(8,128)(2,1)S(1)}, bf16[128,2048]{1,0:T(8,128)(2,1)S(1)}, u32[]{:S(2)}, u32[]{:S(2)}) collective-permute-start(bf16[128,2048]{1,0:T(8,128)(2,1)S(1)} %get-tuple-element.37), channel_id=1, source_target_pairs={{0,24},{8,0},{16,8},{24,16},{1,25},{9,1},{17,9},{25,17},{2,26},{10... | collective-permute-start | bytes 1572872 | tf_op jit(solution)/shard_map/ppermute | solution.py:110
  91.6 0.6 collective-permute-start.7
  92.2 11.7 %collective-permute-done.19.refs_1_ = bf16[128,2048]{1,0:T(8,128)(2,1)S(1)} collective-permute-done((bf16[128,2048]{1,0:T(8,128)(2,1)S(1)}, bf16[128,2048]{1,0:T(8,128)(2,1)S(1)}, u32[]{:S(2)}, u32[]{:S(2)}) %collective-permute-start.19) | collective-permute-done | bytes 524320 | tf_op jit(solution)/shard_map/ppermute | solution.py:110
  104.0 2.9 %collective-permute-start.8 = (bf16[128,2048]{1,0:T(8,128)(2,1)S(1)}, bf16[128,2048]{1,0:T(8,128)(2,1)S(1)}, u32[]{:S(2)}, u32[]{:S(2)}) collective-permute-start(bf16[128,2048]{1,0:T(8,128)(2,1)S(1)} %get-tuple-element.39), channel_id=1, source_target_pairs={{0,8},{8,16},{16,24},{24,0},{1,9},{9,17},{17,25},{25,1},{2,10},{10... | collective-permute-start | bytes 1572872 | tf_op jit(solution)/shard_map/ppermute | solution.py:110
  106.9 0.7 shard_map.70
  107.6 0.7 collective-permute-start.24
  108.3 3.0 %collective-permute-start.23 = (bf16[64,2048]{1,0:T(8,128)(2,1)S(1)}, bf16[64,2048]{1,0:T(8,128)(2,1)S(1)}, u32[]{:S(2)}, u32[]{:S(2)}) collective-permute-start(bf16[64,2048]{1,0:T(8,128)(2,1)S(1)} %get-tuple-element.55), channel_id=1, source_target_pairs={{0,16},{8,24},{16,0},{24,8},{1,17},{9,25},{17,1},{25,9},{2,18},{10... | collective-permute-start | bytes 786440 | tf_op jit(solution)/shard_map/ppermute | solution.py:110
  111.3 8.7 %collective-permute-done.6.refs_1_ = bf16[128,2048]{1,0:T(8,128)(2,1)S(1)} collective-permute-done((bf16[128,2048]{1,0:T(8,128)(2,1)S(1)}, bf16[128,2048]{1,0:T(8,128)(2,1)S(1)}, u32[]{:S(2)}, u32[]{:S(2)}) %collective-permute-start.6) | collective-permute-done | bytes 524320 | tf_op jit(solution)/shard_map/ppermute | solution.py:110
  119.9 3.7 %collective-permute-start.22 = (bf16[64,2048]{1,0:T(8,128)(2,1)S(1)}, bf16[64,2048]{1,0:T(8,128)(2,1)S(1)}, u32[]{:S(2)}, u32[]{:S(2)}) collective-permute-start(bf16[64,2048]{1,0:T(8,128)(2,1)S(1)} %get-tuple-element.54), channel_id=1, source_target_pairs={{0,24},{8,0},{16,8},{24,16},{1,25},{9,1},{17,9},{25,17},{2,26},{10... | collective-permute-start | bytes 786440 | tf_op jit(solution)/shard_map/ppermute | solution.py:110
  123.6 0.7 shard_map.67
  124.3 0.1 collective-permute-start.11
  124.4 2.7 %collective-permute-start.10 = (bf16[64,2048]{1,0:T(8,128)(2,1)S(1)}, bf16[64,2048]{1,0:T(8,128)(2,1)S(1)}, u32[]{:S(2)}, u32[]{:S(2)}) collective-permute-start(bf16[64,2048]{1,0:T(8,128)(2,1)S(1)} %get-tuple-element.42), channel_id=1, source_target_pairs={{0,64},{32,96},{64,0},{96,32},{1,65},{33,97},{65,1},{97,33},{2,66}... | collective-permute-start | bytes 786440 | tf_op jit(solution)/shard_map/ppermute | solution.py:110
  127.1 0.0 collective-permute-done.24
  127.1 1.3 collective-permute-start.9
  128.4 3.7 %collective-permute-done.23 = bf16[64,2048]{1,0:T(8,128)(2,1)S(1)} collective-permute-done((bf16[64,2048]{1,0:T(8,128)(2,1)S(1)}, bf16[64,2048]{1,0:T(8,128)(2,1)S(1)}, u32[]{:S(2)}, u32[]{:S(2)}) %collective-permute-start.23) | collective-permute-done | bytes 262176 | tf_op jit(solution)/shard_map/ppermute | solution.py:110
  132.0 0.0 collective-permute-done.22
  132.1 0.1 add_convert_fusion.1
  132.2 1.5 %collective-permute-start.25 = (bf16[64,2048]{1,0:T(8,128)(2,1)S(1)}, bf16[64,2048]{1,0:T(8,128)(2,1)S(1)}, u32[]{:S(2)}, u32[]{:S(2)}) collective-permute-start(bf16[64,2048]{1,0:T(8,128)(2,1)S(1)} %add_convert_fusion.1), channel_id=1, source_target_pairs={{0,128},{128,0},{1,129},{129,1},{2,130},{130,2},{3,131},{131,3},{4... | collective-permute-start | bytes 786440 | tf_op jit(solution)/shard_map/ppermute | solution.py:110
  133.7 0.0 collective-permute-done.11
  133.7 0.0 collective-permute-done.10
  133.7 2.4 %collective-permute-done.9 = bf16[64,2048]{1,0:T(8,128)(2,1)S(1)} collective-permute-done((bf16[64,2048]{1,0:T(8,128)(2,1)S(1)}, bf16[64,2048]{1,0:T(8,128)(2,1)S(1)}, u32[]{:S(2)}, u32[]{:S(2)}) %collective-permute-start.9) | collective-permute-done | bytes 262176 | tf_op jit(solution)/shard_map/ppermute | solution.py:110
  136.1 2.7 %collective-permute-done.25 = bf16[64,2048]{1,0:T(8,128)(2,1)S(1)} collective-permute-done((bf16[64,2048]{1,0:T(8,128)(2,1)S(1)}, bf16[64,2048]{1,0:T(8,128)(2,1)S(1)}, u32[]{:S(2)}, u32[]{:S(2)}) %collective-permute-start.25) | collective-permute-done | bytes 262176 | tf_op jit(solution)/shard_map/ppermute | solution.py:110
  138.8 0.9 add_convert_fusion
  (17 shorter events, 0.1 us)
Async XLA Ops:
  2.1 0.9 copy-start.6
  3.4 8.6 %collective-permute-start.12 = (bf16[64,2176]{1,0:T(8,128)(2,1)S(1)}, bf16[64,2176]{1,0:T(8,128)(2,1)S(1)}, u32[]{:S(2)}, u32[]{:S(2)}) collective-permute-start(bf16[64,2176]{1,0:T(8,128)(2,1)S(1)} %shard_map.64.refs_0_), channel_id=1, source_target_pairs={{0,128},{128,0},{1,129},{129,1},{2,130},{130,2},{3,131},{131,3},{4... | collective-permute-start | bytes 835592 | tf_op jit(solution)/shard_map/ppermute | solution.py:110
  12.1 9.8 %collective-permute-start.13 = (bf16[64,2176]{1,0:T(8,128)(2,1)S(1)}, bf16[64,2176]{1,0:T(8,128)(2,1)S(1)}, u32[]{:S(2)}, u32[]{:S(2)}) collective-permute-start(bf16[64,2176]{1,0:T(8,128)(2,1)S(1)} %collective-permute-done.12.refs_0_), channel_id=1, source_target_pairs={{0,8},{8,16},{16,24},{24,0},{1,9},{9,17},{17,25},{25,1},{2,10},{10... | collective-permute-start | bytes 835592 | tf_op jit(solution)/shard_map/ppermute | solution.py:110
  13.5 14.4 %collective-permute-start.14 = (bf16[64,2176]{1,0:T(8,128)(2,1)S(1)}, bf16[64,2176]{1,0:T(8,128)(2,1)S(1)}, u32[]{:S(2)}, u32[]{:S(2)}) collective-permute-start(bf16[64,2176]{1,0:T(8,128)(2,1)S(1)} %collective-permute-done.12.refs_0_), channel_id=1, source_target_pairs={{0,16},{8,24},{16,0},{24,8},{1,17},{9,25},{17,1},{25,9},{2,18},{10... | collective-permute-start | bytes 835592 | tf_op jit(solution)/shard_map/ppermute | solution.py:110
  16.3 11.7 %collective-permute-start.15 = (bf16[64,2176]{1,0:T(8,128)(2,1)S(1)}, bf16[64,2176]{1,0:T(8,128)(2,1)S(1)}, u32[]{:S(2)}, u32[]{:S(2)}) collective-permute-start(bf16[64,2176]{1,0:T(8,128)(2,1)S(1)} %collective-permute-done.12.refs_0_), channel_id=1, source_target_pairs={{0,24},{8,0},{16,8},{24,16},{1,25},{9,1},{17,9},{25,17},{2,26},{10... | collective-permute-start | bytes 835592 | tf_op jit(solution)/shard_map/ppermute | solution.py:110
  17.7 19.1 %collective-permute-start = (bf16[64,2176]{1,0:T(8,128)(2,1)S(1)}, bf16[64,2176]{1,0:T(8,128)(2,1)S(1)}, u32[]{:S(2)}, u32[]{:S(2)}) collective-permute-start(bf16[64,2176]{1,0:T(8,128)(2,1)S(1)} %shard_map.64.refs_0_), channel_id=1, source_target_pairs={{0,32},{32,64},{64,96},{96,0},{1,33},{33,65},{65,97},{97,1},{2,34}... | collective-permute-start | bytes 835592 | tf_op jit(solution)/shard_map/ppermute | solution.py:110
  30.6 29.1 %collective-permute-start.16 = (bf16[128,2048]{1,0:T(8,128)(2,1)}, bf16[128,2048]{1,0:T(8,128)(2,1)S(1)}, u32[]{:S(2)}, u32[]{:S(2)}) collective-permute-start(bf16[128,2048]{1,0:T(8,128)(2,1)} %get-tuple-element.46), channel_id=1, source_target_pairs={{0,32},{32,64},{64,96},{96,0},{1,33},{33,65},{65,97},{97,1},{2,34}... | collective-permute-start | bytes 1572872 | tf_op jit(solution)/shard_map/ppermute | solution.py:110
  30.8 11.0 %collective-permute-start.1 = (bf16[64,2176]{1,0:T(8,128)(2,1)S(1)}, bf16[64,2176]{1,0:T(8,128)(2,1)S(1)}, u32[]{:S(2)}, u32[]{:S(2)}) collective-permute-start(bf16[64,2176]{1,0:T(8,128)(2,1)S(1)} %shard_map.64.refs_0_), channel_id=1, source_target_pairs={{0,64},{32,96},{64,0},{96,32},{1,65},{33,97},{65,1},{97,33},{2,66}... | collective-permute-start | bytes 835592 | tf_op jit(solution)/shard_map/ppermute | solution.py:110
  33.4 22.0 %collective-permute-start.2 = (bf16[64,2176]{1,0:T(8,128)(2,1)S(1)}, bf16[64,2176]{1,0:T(8,128)(2,1)S(1)}, u32[]{:S(2)}, u32[]{:S(2)}) collective-permute-start(bf16[64,2176]{1,0:T(8,128)(2,1)S(1)} %shard_map.64.refs_0_), channel_id=1, source_target_pairs={{0,96},{32,0},{64,32},{96,64},{1,97},{33,1},{65,33},{97,65},{2,98}... | collective-permute-start | bytes 835592 | tf_op jit(solution)/shard_map/ppermute | solution.py:110
  33.4 28.8 %collective-permute-start.17 = (bf16[128,2048]{1,0:T(8,128)(2,1)}, bf16[128,2048]{1,0:T(8,128)(2,1)S(1)}, u32[]{:S(2)}, u32[]{:S(2)}) collective-permute-start(bf16[128,2048]{1,0:T(8,128)(2,1)} %get-tuple-element.47), channel_id=1, source_target_pairs={{0,64},{32,96},{64,0},{96,32},{1,65},{33,97},{65,1},{97,33},{2,66}... | collective-permute-start | bytes 1572872 | tf_op jit(solution)/shard_map/ppermute | solution.py:110
  36.8 30.8 %collective-permute-start.18 = (bf16[128,2048]{1,0:T(8,128)(2,1)}, bf16[128,2048]{1,0:T(8,128)(2,1)S(1)}, u32[]{:S(2)}, u32[]{:S(2)}) collective-permute-start(bf16[128,2048]{1,0:T(8,128)(2,1)} %get-tuple-element.48), channel_id=1, source_target_pairs={{0,96},{32,0},{64,32},{96,64},{1,97},{33,1},{65,33},{97,65},{2,98}... | collective-permute-start | bytes 1572872 | tf_op jit(solution)/shard_map/ppermute | solution.py:110
  56.9 23.6 %collective-permute-start.3 = (bf16[128,2048]{1,0:T(8,128)(2,1)S(1)}, bf16[128,2048]{1,0:T(8,128)(2,1)S(1)}, u32[]{:S(2)}, u32[]{:S(2)}) collective-permute-start(bf16[128,2048]{1,0:T(8,128)(2,1)S(1)} %get-tuple-element.33), channel_id=1, source_target_pairs={{0,8},{8,16},{16,24},{24,0},{1,9},{9,17},{17,25},{25,1},{2,10},{10... | collective-permute-start | bytes 1572872 | tf_op jit(solution)/shard_map/ppermute | solution.py:110
  57.0 25.8 %collective-permute-start.4 = (bf16[128,2048]{1,0:T(8,128)(2,1)S(1)}, bf16[128,2048]{1,0:T(8,128)(2,1)S(1)}, u32[]{:S(2)}, u32[]{:S(2)}) collective-permute-start(bf16[128,2048]{1,0:T(8,128)(2,1)S(1)} %get-tuple-element.34), channel_id=1, source_target_pairs={{0,16},{8,24},{16,0},{24,8},{1,17},{9,25},{17,1},{25,9},{2,18},{10... | collective-permute-start | bytes 1572872 | tf_op jit(solution)/shard_map/ppermute | solution.py:110
  59.7 23.1 %collective-permute-start.5 = (bf16[128,2048]{1,0:T(8,128)(2,1)S(1)}, bf16[128,2048]{1,0:T(8,128)(2,1)S(1)}, u32[]{:S(2)}, u32[]{:S(2)}) collective-permute-start(bf16[128,2048]{1,0:T(8,128)(2,1)S(1)} %get-tuple-element.35), channel_id=1, source_target_pairs={{0,24},{8,0},{16,8},{24,16},{1,25},{9,1},{17,9},{25,17},{2,26},{10... | collective-permute-start | bytes 1572872 | tf_op jit(solution)/shard_map/ppermute | solution.py:110
  67.6 1.9 %copy-start = (bf16[1,2048,768]{2,1,0:T(8,128)(2,1)S(1)}, bf16[1,2048,768]{2,1,0:T(8,128)(2,1)}, u32[]{:S(2)}) copy-start(bf16[1,2048,768]{2,1,0:T(8,128)(2,1)} %gate_ref.3) | copy-start | bytes 9437188
  69.5 1.9 %copy-start.2 = (bf16[1,2048,768]{2,1,0:T(8,128)(2,1)S(1)}, bf16[1,2048,768]{2,1,0:T(8,128)(2,1)}, u32[]{:S(2)}) copy-start(bf16[1,2048,768]{2,1,0:T(8,128)(2,1)} %up_ref.3) | copy-start | bytes 9437188
  71.4 1.9 %copy-start.4 = (bf16[1,768,2048]{2,1,0:T(8,128)(2,1)S(1)}, bf16[1,768,2048]{2,1,0:T(8,128)(2,1)}, u32[]{:S(2)}) copy-start(bf16[1,768,2048]{2,1,0:T(8,128)(2,1)} %down_ref.3) | copy-start | bytes 9437188
  73.3 9.5 %copy-start.1 = (bf16[1,2048,768]{2,1,0:T(8,128)(2,1)S(1)}, bf16[1,2048,768]{2,1,0:T(8,128)(2,1)}, u32[]{:S(2)}) copy-start(bf16[1,2048,768]{2,1,0:T(8,128)(2,1)} %gate_ref.3) | copy-start | bytes 9437188
  73.3 9.5 %copy-start.3 = (bf16[1,2048,768]{2,1,0:T(8,128)(2,1)S(1)}, bf16[1,2048,768]{2,1,0:T(8,128)(2,1)}, u32[]{:S(2)}) copy-start(bf16[1,2048,768]{2,1,0:T(8,128)(2,1)} %up_ref.3) | copy-start | bytes 9437188
  73.3 9.5 %copy-start.5 = (bf16[1,768,2048]{2,1,0:T(8,128)(2,1)S(1)}, bf16[1,768,2048]{2,1,0:T(8,128)(2,1)}, u32[]{:S(2)}) copy-start(bf16[1,768,2048]{2,1,0:T(8,128)(2,1)} %down_ref.3) | copy-start | bytes 9437188
  78.3 25.6 %collective-permute-start.19 = (bf16[128,2048]{1,0:T(8,128)(2,1)S(1)}, bf16[128,2048]{1,0:T(8,128)(2,1)S(1)}, u32[]{:S(2)}, u32[]{:S(2)}) collective-permute-start(bf16[128,2048]{1,0:T(8,128)(2,1)S(1)} %get-tuple-element.50), channel_id=1, source_target_pairs={{0,96},{32,0},{64,32},{96,64},{1,97},{33,1},{65,33},{97,65},{2,98}... | collective-permute-start | bytes 1572872 | tf_op jit(solution)/shard_map/ppermute | solution.py:110
  79.5 27.4 %collective-permute-start.20 = (bf16[128,2048]{1,0:T(8,128)(2,1)S(1)}, bf16[128,2048]{1,0:T(8,128)(2,1)S(1)}, u32[]{:S(2)}, u32[]{:S(2)}) collective-permute-start(bf16[128,2048]{1,0:T(8,128)(2,1)S(1)} %get-tuple-element.51), channel_id=1, source_target_pairs={{0,64},{32,96},{64,0},{96,32},{1,65},{33,97},{65,1},{97,33},{2,66}... | collective-permute-start | bytes 1572872 | tf_op jit(solution)/shard_map/ppermute | solution.py:110
  80.4 26.4 %collective-permute-start.21 = (bf16[128,2048]{1,0:T(8,128)(2,1)S(1)}, bf16[128,2048]{1,0:T(8,128)(2,1)S(1)}, u32[]{:S(2)}, u32[]{:S(2)}) collective-permute-start(bf16[128,2048]{1,0:T(8,128)(2,1)S(1)} %get-tuple-element.52), channel_id=1, source_target_pairs={{0,32},{32,64},{64,96},{96,0},{1,33},{33,65},{65,97},{97,1},{2,34}... | collective-permute-start | bytes 1572872 | tf_op jit(solution)/shard_map/ppermute | solution.py:110
  87.9 32.0 %collective-permute-start.6 = (bf16[128,2048]{1,0:T(8,128)(2,1)S(1)}, bf16[128,2048]{1,0:T(8,128)(2,1)S(1)}, u32[]{:S(2)}, u32[]{:S(2)}) collective-permute-start(bf16[128,2048]{1,0:T(8,128)(2,1)S(1)} %get-tuple-element.37), channel_id=1, source_target_pairs={{0,24},{8,0},{16,8},{24,16},{1,25},{9,1},{17,9},{25,17},{2,26},{10... | collective-permute-start | bytes 1572872 | tf_op jit(solution)/shard_map/ppermute | solution.py:110
  91.6 32.0 %collective-permute-start.7 = (bf16[128,2048]{1,0:T(8,128)(2,1)S(1)}, bf16[128,2048]{1,0:T(8,128)(2,1)S(1)}, u32[]{:S(2)}, u32[]{:S(2)}) collective-permute-start(bf16[128,2048]{1,0:T(8,128)(2,1)S(1)} %get-tuple-element.38), channel_id=1, source_target_pairs={{0,16},{8,24},{16,0},{24,8},{1,17},{9,25},{17,1},{25,9},{2,18},{10... | collective-permute-start | bytes 1572872 | tf_op jit(solution)/shard_map/ppermute | solution.py:110
  104.0 19.7 %collective-permute-start.8 = (bf16[128,2048]{1,0:T(8,128)(2,1)S(1)}, bf16[128,2048]{1,0:T(8,128)(2,1)S(1)}, u32[]{:S(2)}, u32[]{:S(2)}) collective-permute-start(bf16[128,2048]{1,0:T(8,128)(2,1)S(1)} %get-tuple-element.39), channel_id=1, source_target_pairs={{0,8},{8,16},{16,24},{24,0},{1,9},{9,17},{17,25},{25,1},{2,10},{10... | collective-permute-start | bytes 1572872 | tf_op jit(solution)/shard_map/ppermute | solution.py:110
  107.6 19.5 %collective-permute-start.24 = (bf16[64,2048]{1,0:T(8,128)(2,1)S(1)}, bf16[64,2048]{1,0:T(8,128)(2,1)S(1)}, u32[]{:S(2)}, u32[]{:S(2)}) collective-permute-start(bf16[64,2048]{1,0:T(8,128)(2,1)S(1)} %get-tuple-element.56), channel_id=1, source_target_pairs={{0,8},{8,16},{16,24},{24,0},{1,9},{9,17},{17,25},{25,1},{2,10},{10... | collective-permute-start | bytes 786440 | tf_op jit(solution)/shard_map/ppermute | solution.py:110
  108.3 23.8 %collective-permute-start.23 = (bf16[64,2048]{1,0:T(8,128)(2,1)S(1)}, bf16[64,2048]{1,0:T(8,128)(2,1)S(1)}, u32[]{:S(2)}, u32[]{:S(2)}) collective-permute-start(bf16[64,2048]{1,0:T(8,128)(2,1)S(1)} %get-tuple-element.55), channel_id=1, source_target_pairs={{0,16},{8,24},{16,0},{24,8},{1,17},{9,25},{17,1},{25,9},{2,18},{10... | collective-permute-start | bytes 786440 | tf_op jit(solution)/shard_map/ppermute | solution.py:110
  119.9 12.1 %collective-permute-start.22 = (bf16[64,2048]{1,0:T(8,128)(2,1)S(1)}, bf16[64,2048]{1,0:T(8,128)(2,1)S(1)}, u32[]{:S(2)}, u32[]{:S(2)}) collective-permute-start(bf16[64,2048]{1,0:T(8,128)(2,1)S(1)} %get-tuple-element.54), channel_id=1, source_target_pairs={{0,24},{8,0},{16,8},{24,16},{1,25},{9,1},{17,9},{25,17},{2,26},{10... | collective-permute-start | bytes 786440 | tf_op jit(solution)/shard_map/ppermute | solution.py:110
  124.3 9.3 %collective-permute-start.11 = (bf16[64,2048]{1,0:T(8,128)(2,1)S(1)}, bf16[64,2048]{1,0:T(8,128)(2,1)S(1)}, u32[]{:S(2)}, u32[]{:S(2)}) collective-permute-start(bf16[64,2048]{1,0:T(8,128)(2,1)S(1)} %get-tuple-element.43), channel_id=1, source_target_pairs={{0,32},{32,64},{64,96},{96,0},{1,33},{33,65},{65,97},{97,1},{2,34}... | collective-permute-start | bytes 786440 | tf_op jit(solution)/shard_map/ppermute | solution.py:110
  124.4 9.3 %collective-permute-start.10 = (bf16[64,2048]{1,0:T(8,128)(2,1)S(1)}, bf16[64,2048]{1,0:T(8,128)(2,1)S(1)}, u32[]{:S(2)}, u32[]{:S(2)}) collective-permute-start(bf16[64,2048]{1,0:T(8,128)(2,1)S(1)} %get-tuple-element.42), channel_id=1, source_target_pairs={{0,64},{32,96},{64,0},{96,32},{1,65},{33,97},{65,1},{97,33},{2,66}... | collective-permute-start | bytes 786440 | tf_op jit(solution)/shard_map/ppermute | solution.py:110
  127.1 9.0 %collective-permute-start.9 = (bf16[64,2048]{1,0:T(8,128)(2,1)S(1)}, bf16[64,2048]{1,0:T(8,128)(2,1)S(1)}, u32[]{:S(2)}, u32[]{:S(2)}) collective-permute-start(bf16[64,2048]{1,0:T(8,128)(2,1)S(1)} %get-tuple-element.41), channel_id=1, source_target_pairs={{0,96},{32,0},{64,32},{96,64},{1,97},{33,1},{65,33},{97,65},{2,98}... | collective-permute-start | bytes 786440 | tf_op jit(solution)/shard_map/ppermute | solution.py:110
  132.2 6.6 %collective-permute-start.25 = (bf16[64,2048]{1,0:T(8,128)(2,1)S(1)}, bf16[64,2048]{1,0:T(8,128)(2,1)S(1)}, u32[]{:S(2)}, u32[]{:S(2)}) collective-permute-start(bf16[64,2048]{1,0:T(8,128)(2,1)S(1)} %add_convert_fusion.1), channel_id=1, source_target_pairs={{0,128},{128,0},{1,129},{129,1},{2,130},{130,2},{3,131},{131,3},{4... | collective-permute-start | bytes 786440 | tf_op jit(solution)/shard_map/ppermute | solution.py:110
